TPU v7x, 256 devices: a whole 4x4x8 slice. The times are simulated.
256 devices in a mesh: row: 16 (over y_lo, x, core), col: 16 (over z, y_hi).
Axes of the slice: x: 4, y: 4 (y_hi: 2, y_lo: 2; y = y_hi * 2 + y_lo), z: 8, core: 2. Of those that a mesh axis runs over, the one named last changes fastest.
Arguments:
- tokens: bfloat16 [16, 16, 736, 1024], P('row', 'col'), may hold values from -6 to 6
- local_params: bfloat16 [16, 16, 2, 1024, 1024], P('row', 'col'), may hold values from -0.1875 to 0.1875
- outer_params: float32 [2, 16, 16, 16, 4, 1024], P(None, None, 'col', 'row'), may hold values from -0.1875 to 0.1875
- momentum: float32 [2, 16, 16, 16, 4, 1024], P(None, None, 'col', 'row'), may hold values from -0.1875 to 0.1875
- table: int32 [16, 16], replicated, may hold values from 0 to 15, each once within a row
- counts: int32 [16, 16], replicated, may hold values from 64 to 4095
Outputs:
- path_params: bfloat16 [16, 16, 2, 1024, 1024], P('row', 'col')
- outer_out: float32 [2, 16, 16, 16, 4, 1024], P(None, None, 'col', 'row')
- momentum_out: float32 [2, 16, 16, 16, 4, 1024], P(None, None, 'col', 'row')
- hidden_out: bfloat16 [16, 16, 736, 1024], P('row', 'col')
Inputs may be any that keep to these rules, and one draw needn't show every extreme that they name: Each row of the table names every level-two module exactly once.
All inputs are finite; a program needn't handle non-finite values.
Results may differ from a plain program's by a relative error of at most 0.01.
Values may be sent and summed in bfloat16 or wider, within the bound.
No kernel may reach another device: no remote copies, remote signals or barrier semaphores. Data moves between devices by JAX's collectives and lax.ppermute only.
A program may use at most 64 MiB of HBM per device.

v0:
```python
import jax
import jax.numpy as jnp
from jax import lax
from jax.sharding import PartitionSpec as P


def cut_along(shard, dim, count):
    before, after = (shard.shape[:dim], shard.shape[dim + 1 :])
    return jnp.moveaxis(shard.reshape(*before, count, -1, *after), dim, 0)


def sum_at_owner(shard, axis, dim):
    blocks = cut_along(shard, dim, lax.axis_size(axis))
    arrived = lax.all_to_all(blocks, axis, split_axis=0, concat_axis=0, tiled=True)
    return arrived.astype(jnp.float32).sum(axis=0)


def outer_round(scaled, outer, moment, my_row, inverse):
    layers = scaled.shape[0]
    width = scaled.shape[-1]
    n_col = lax.axis_size("col")
    pieces = scaled.reshape(layers, n_col, width // n_col, width)
    arrived = lax.all_to_all(pieces, "col", split_axis=1, concat_axis=1, tiled=True)
    ordered = jnp.take(arrived, inverse, axis=1)
    summed = sum_at_owner(ordered, "row", 2)
    delta = outer - summed
    moment_new = 0.9 * moment + delta
    outer_new = outer - 0.7 * (delta + 0.9 * moment_new)
    whole = lax.all_gather(outer_new.astype(jnp.bfloat16), "row", axis=2, tiled=True)
    chosen = jnp.take(whole, my_row, axis=1)
    returned = lax.all_to_all(chosen, "col", split_axis=1, concat_axis=1, tiled=True)
    return (outer_new, moment_new, returned.reshape(layers, width, width))


def micro_step(tokens_path, params_path):
    state = tokens_path.astype(jnp.float32)
    for layer in range(params_path.shape[0]):
        scale = lax.rsqrt(jnp.mean(state * state, axis=-1, keepdims=True) + 1e-06)
        normed = (state * scale).astype(jnp.bfloat16)
        mixed = jnp.dot(normed, params_path[layer], preferred_element_type=jnp.float32)
        state = state + jax.nn.gelu(mixed, approximate=False)
    return state.astype(jnp.bfloat16)


def on_device(tokens, local_params, outer_params, momentum, table, counts):
    row_index = lax.axis_index("row")
    col_index = lax.axis_index("col")
    n_col = table.shape[1]
    ids = jnp.arange(n_col, dtype=jnp.int32)
    matches = (table[:, :, None] == ids[None, None, :]).astype(jnp.float32)
    totals = jnp.sum(counts.astype(jnp.float32)[:, :, None] * matches, axis=(0, 1))
    my_row = lax.dynamic_index_in_dim(table, row_index, 0, keepdims=False)
    count_row = lax.dynamic_index_in_dim(counts, row_index, 0, keepdims=False)
    my_module = lax.dynamic_index_in_dim(my_row, col_index, 0, keepdims=False)
    my_count = lax.dynamic_index_in_dim(count_row, col_index, 0, keepdims=False)
    share = my_count.astype(jnp.float32) / jnp.sum(totals * (ids == my_module).astype(jnp.float32))
    inverse = jnp.sum(ids[:, None] * (my_row[:, None] == ids[None, :]).astype(jnp.int32), axis=0)
    params = local_params[0, 0]
    layers = params.shape[0]
    width = params.shape[-1]
    scaled = (share * params.astype(jnp.float32)).astype(jnp.bfloat16)
    outer = outer_params.reshape(layers, n_col, -1, width)
    moment = momentum.reshape(layers, n_col, -1, width)
    outer_new, moment_new, returned = outer_round(scaled, outer, moment, my_row, inverse)
    hidden = micro_step(tokens[0, 0], params)
    return (
        returned[None, None],
        outer_new.reshape(outer_params.shape),
        moment_new.reshape(momentum.shape),
        hidden[None, None],
    )


def solution(mesh):
    return jax.shard_map(
        on_device,
        mesh=mesh,
        in_specs=(
            P("row", "col", None, None),
            P("row", "col", None, None, None),
            P(None, None, "col", "row", None, None),
            P(None, None, "col", "row", None, None),
            P(),
            P(),
        ),
        out_specs=(
            P("row", "col", None, None, None),
            P(None, None, "col", "row", None, None),
            P(None, None, "col", "row", None, None),
            P("row", "col", None, None),
        ),
        check_vma=False,
    )
```

profile of v0, /device:TPU:1, one launch (start us, length us, event | category | flops | bytes accessed | tf_op | source)
XLA Modules:
  0.0 381.6 jit_solution(6195041350932074072)
XLA Ops:
  7.2 0.7 convert_element_type.53
  7.9 1.3 dynamic_slice.12
  9.1 1.3 dynamic_slice.13
  10.4 0.8 select_reduce_fusion
  11.9 1.2 fusion.49
  13.9 3.3 multiply_convert_fusion
  17.1 2.5 copy.58
  19.6 11.8 %all-to-all-start = ((bf16[2,16,64,1024]{3,2,0,1:T(8,128)(2,1)}), bf16[2,16,64,1024]{3,2,0,1:T(8,128)(2,1)}, u32[]{:S(2)}, u32[]{:S(2)}) async-start(bf16[2,16,64,1024]{3,2,0,1:T(8,128)(2,1)} %copy.58), calls=%async_computation | async-start | bytes 8388608 | tf_op jit(solution)/shard_map/all_to_all | solution.py:23
  31.4 0.0 all-gather.2.cloned.1.call-start
  31.4 0.7 compare_and_fusion
  32.1 0.1 select_reduce_fusion.1
  32.3 97.6 %all-to-all-done = bf16[2,16,64,1024]{3,2,0,1:T(8,128)(2,1)} async-done(((bf16[2,16,64,1024]{3,2,0,1:T(8,128)(2,1)}), bf16[2,16,64,1024]{3,2,0,1:T(8,128)(2,1)}, u32[]{:S(2)}, u32[]{:S(2)}) %all-to-all-start) | async-done | bytes 4194336 | tf_op jit(solution)/shard_map/all_to_all | solution.py:23
  129.9 5.0 %gather_fusion = bf16[16,2,64,1024]{3,2,1,0:T(8,128)(2,1)} fusion(bf16[2,16,64,1024]{3,2,0,1:T(8,128)(2,1)} %all-to-all-done, s32[1024]{0:T(1024)S(1)} %pad_clamp_fusion.1), kind=kCustom, calls=%fused_computation.clone | custom fusion | bytes 8388672 | tf_op jit(solution)/shard_map/jit(_take)/gather | solution.py:24
  134.9 4.7 %select_bitcast_fusion.1 = bf16[2,16,64,1024]{3,2,0,1:T(8,128)(2,1)} fusion(bf16[16,2,64,1024]{3,2,1,0:T(8,128)(2,1)} %gather_fusion, pred[16]{0:T(512)(128)(4,1)S(1)} %compare_and_fusion.1), kind=kLoop, calls=%fused_computation.8 | loop fusion | flops 2097152 | bytes 8388624 | tf_op jit(solution)/shard_map/jit(_take)/select_n | solution.py:24
  139.6 7.2 %reshape.72 = bf16[2,16,16,4,1024]{4,3,2,0,1:T(4,128)(2,1)} reshape(bf16[2,16,64,1024]{3,2,0,1:T(8,128)(2,1)} %select_bitcast_fusion.1) | data formatting | bytes 8388608 | tf_op jit(solution)/shard_map/reshape | solution.py:9
  146.8 4.6 %copy.93 = bf16[2,16,16,4,1024]{4,3,0,1,2:T(4,128)(2,1)S(1)} copy(bf16[2,16,16,4,1024]{4,3,2,0,1:T(4,128)(2,1)} %reshape.72) | data formatting | bytes 8388608 | tf_op jit(solution)/shard_map/reshape | solution.py:9
  151.3 54.5 %all_to_all.15 = bf16[16,2,16,4,1024]{4,3,1,2,0:T(4,128)(2,1)S(1)} all-to-all(bf16[16,2,16,4,1024]{4,3,1,2,0:T(4,128)(2,1)S(1)} %bitcast.75), channel_id=1, replica_groups=mesh['row'=16,'col'=16] {'row'}, dimensions={0} | all-to-all | bytes 8388608 | tf_op jit(solution)/shard_map/all_to_all | solution.py:14
  205.8 0.0 copy-start.1
  205.8 0.0 copy-start.2
  205.8 2.2 convert_reduce_fusion
  208.1 0.0 copy-done.1
  208.1 0.0 copy-done.2
  208.1 0.6 fusion.47
  208.7 0.9 copy.63
  209.6 0.0 all-gather.2.cloned.1.call-update
  209.7 35.8 %all-gather.2.cloned.1.call-done = bf16[2,16,64,1024]{3,1,0,2:T(8,128)(2,1)} async-done(((bf16[2,16,4,1024]{3,1,0,2:T(8,128)(2,1)}), bf16[2,16,64,1024]{3,1,0,2:T(8,128)(2,1)}) %all-gather.2.cloned.1.call-update) | async-done | bytes 4194320 | tf_op jit(solution)/shard_map/all_gather | solution.py:29
  245.5 6.5 %copy.64 = bf16[2,16,64,1024]{3,2,1,0:T(8,128)(2,1)} copy(bf16[2,16,64,1024]{3,1,0,2:T(8,128)(2,1)} %all-gather.2.cloned.1.call-done) | data formatting | bytes 8388608 | tf_op jit(solution)/shard_map/all_gather | solution.py:29
  252.0 4.9 %gather_fusion.1 = bf16[16,2,64,1024]{3,2,1,0:T(8,128)(2,1)} fusion(bf16[2,16,64,1024]{3,2,1,0:T(8,128)(2,1)} %copy.64, s32[1024]{0:T(1024)S(1)} %pad_clamp_fusion), kind=kCustom, calls=%fused_computation.1.clone | custom fusion | bytes 8388672 | tf_op jit(solution)/shard_map/jit(_take)/gather | solution.py:30
  256.9 4.7 %select_bitcast_fusion = bf16[2,16,64,1024]{3,2,0,1:T(8,128)(2,1)} fusion(bf16[16,2,64,1024]{3,2,1,0:T(8,128)(2,1)} %gather_fusion.1, pred[16]{0:T(512)(128)(4,1)S(1)} %get-tuple-element.25), kind=kLoop, calls=%fused_computation.7 | loop fusion | flops 2097152 | bytes 8388624 | tf_op jit(solution)/shard_map/jit(_take)/select_n | solution.py:30
  261.6 0.0 copy-start.3
  261.6 9.2 %all-to-all-start.2 = ((bf16[2,16,64,1024]{3,2,0,1:T(8,128)(2,1)}), bf16[2,16,64,1024]{3,2,0,1:T(8,128)(2,1)}, u32[]{:S(2)}, u32[]{:S(2)}) async-start(bf16[2,16,64,1024]{3,2,0,1:T(8,128)(2,1)} %select_bitcast_fusion), calls=%async_computation.2 | async-start | bytes 8388608 | tf_op jit(solution)/shard_map/all_to_all | solution.py:31
  270.8 0.0 copy-done.3
  270.8 0.4 fusion.2
  271.2 0.0 copy-start
  271.2 10.1 %multiply_reduce_fusion = (f32[736]{0:T(1024)S(1)}, f32[736,1024]{1,0:T(8,128)S(1)}) fusion(bf16[1,1,2,1024,1024]{4,3,2,1,0:T(8,128)(2,1)} %param.9, bf16[1,1,736,1024]{3,2,1,0:T(8,128)(2,1)S(1)} %copy-done.3, f32[736]{0:T(1024)S(1)} %add_rsqrt_fusion.1), kind=kOutput, calls=%fused_computation.35 | convolution fusion | flops 1597013248 | bytes 8133504 | tf_op jit(solution)/shard_map/dot_general | solution.py:40
  281.3 0.0 copy-done
  281.3 9.4 %fusion.36 = bf16[1,1,736,1024]{3,2,1,0:T(8,128)(2,1)} fusion(f32[736,1024]{1,0:T(8,128)S(1)} %get-tuple-element.30, bf16[1,1,2,1024,1024]{4,3,2,1,0:T(8,128)(2,1)S(1)} %copy-done, f32[736]{0:T(1024)S(1)} %add_rsqrt_fusion), kind=kOutput, calls=%fused_computation.62 | convolution fusion | flops 1594753024 | bytes 9637888 | tf_op jit(solution)/shard_map/dot_general | solution.py:40
  290.7 0.7 fusion.48
  291.4 0.8 copy.68
  292.2 0.8 copy.69
  293.0 76.8 %all-to-all-done.2 = bf16[2,16,64,1024]{3,2,0,1:T(8,128)(2,1)} async-done(((bf16[2,16,64,1024]{3,2,0,1:T(8,128)(2,1)}), bf16[2,16,64,1024]{3,2,0,1:T(8,128)(2,1)}, u32[]{:S(2)}, u32[]{:S(2)}) %all-to-all-start.2) | async-done | bytes 4194336 | tf_op jit(solution)/shard_map/all_to_all | solution.py:31
  369.8 4.9 %copy.65 = bf16[2,16,64,1024]{3,2,1,0:T(8,128)(2,1)} copy(bf16[2,16,64,1024]{3,2,0,1:T(8,128)(2,1)} %all-to-all-done.2) | data formatting | bytes 8388608 | tf_op jit(solution)/shard_map/all_to_all | solution.py:31
  (7 shorter events, 0.0 us)
Async XLA Ops:
  19.6 110.3 %all-to-all-start = ((bf16[2,16,64,1024]{3,2,0,1:T(8,128)(2,1)}), bf16[2,16,64,1024]{3,2,0,1:T(8,128)(2,1)}, u32[]{:S(2)}, u32[]{:S(2)}) async-start(bf16[2,16,64,1024]{3,2,0,1:T(8,128)(2,1)} %copy.58), calls=%async_computation | async-start | bytes 8388608 | tf_op jit(solution)/shard_map/all_to_all | solution.py:23
  31.4 214.1 %all-gather.2.cloned.1.call-start = ((), (), s32[]{:S(2)}) async-start(), calls=%async_computation.3 | async-start | bytes 4456448 | tf_op jit(solution)/shard_map/all_gather | solution.py:29
  205.8 2.3 copy-start.1
  205.8 2.3 copy-start.2
  261.6 9.3 %copy-start.3 = (bf16[1,1,736,1024]{3,2,1,0:T(8,128)(2,1)S(1)}, bf16[1,1,736,1024]{3,2,1,0:T(8,128)(2,1)}, u32[]{:S(2)}) copy-start(bf16[1,1,736,1024]{3,2,1,0:T(8,128)(2,1)} %param.8) | copy-start | bytes 4521988
  261.6 108.2 %all-to-all-start.2 = ((bf16[2,16,64,1024]{3,2,0,1:T(8,128)(2,1)}), bf16[2,16,64,1024]{3,2,0,1:T(8,128)(2,1)}, u32[]{:S(2)}, u32[]{:S(2)}) async-start(bf16[2,16,64,1024]{3,2,0,1:T(8,128)(2,1)} %select_bitcast_fusion), calls=%async_computation.2 | async-start | bytes 8388608 | tf_op jit(solution)/shard_map/all_to_all | solution.py:31
  271.2 10.1 %copy-start = (bf16[1,1,2,1024,1024]{4,3,2,1,0:T(8,128)(2,1)S(1)}, bf16[1,1,2,1024,1024]{4,3,2,1,0:T(8,128)(2,1)}, u32[]{:S(2)}) copy-start(bf16[1,1,2,1024,1024]{4,3,2,1,0:T(8,128)(2,1)} %param.9) | copy-start | bytes 12582916
Sparse Core Ops, SparseCore 0:
  209.7 35.6 all-gather.1
where the time goes:
time: 382 us
  waiting for transfers between devices  210 us (55%)
  blocking collectives  54.5 us (14%)
  local copies, waits for them, and re-layouts  40.7 us (11%)
  starting transfers between devices  21.1 us (6%)
  other arithmetic  20.2 us (5%)
  matrix products  19.5 us (5%)
  between operations  15.5 us (4%)
    all_to_all x1, waiting for transfers between devices, outer_round(): lax.all_to_all(pieces, 'col', split_axis=1, concat_axis=1, tiled=True)  97.6 us
    all_to_all x1, waiting for transfers between devices, outer_round(): lax.all_to_all(chosen, 'col', split_axis=1, concat_axis=1, tiled=True)  76.8 us
    all_to_all x1, blocking collectives, sum_at_owner(): lax.all_to_all(blocks, axis, split_axis=0, concat_axis=0, tiled=True)  54.5 us
    all_gather x1, waiting for transfers between devices, outer_round(): lax.all_gather(outer_new.astype(jnp.bfloat16), 'row', axis=2, tiled=True)  35.8 us
    dot_general x2, matrix products, micro_step(): jnp.dot(normed, params_path[layer], preferred_element_type=jnp.float32)  19.5 us
    all_to_all x1, starting transfers between devices, outer_round(): lax.all_to_all(pieces, 'col', split_axis=1, concat_axis=1, tiled=True)  11.8 us
    reshape x2, local copies, waits for them, and re-layouts, cut_along(): return jnp.moveaxis(shard.reshape(*before, count, -1, *after), dim, 0)  11.8 us
    all_to_all x1, starting transfers between devices, outer_round(): lax.all_to_all(chosen, 'col', split_axis=1, concat_axis=1, tiled=True)  9.24 us
  transfers between devices with their start and end apart: 3, of which 3 were waited for; matrix products, arithmetic and copies ran while one was open for 6% of the time, Pallas kernels for 0%

commit v1 on v0

--- a/solution.py
+++ b/solution.py
@@ -26,7 +26,7 @@
     delta = outer - summed
     moment_new = 0.9 * moment + delta
     outer_new = outer - 0.7 * (delta + 0.9 * moment_new)
-    whole = lax.all_gather(outer_new.astype(jnp.bfloat16), "row", axis=2, tiled=True)
+    whole = jnp.concatenate(lax.all_gather(outer_new.astype(jnp.bfloat16), "row"), axis=2)
     chosen = jnp.take(whole, my_row, axis=1)
     returned = lax.all_to_all(chosen, "col", split_axis=1, concat_axis=1, tiled=True)
     return (outer_new, moment_new, returned.reshape(layers, width, width))

time: 382 us -> 383 us (level)
    reshape x0 -> x1, local copies, waits for them, and re-layouts: none -> 4.34 us  [outer_round(): jnp.concatenate(lax.all_gather(outer_new.astype(jnp.bfloat16), 'row'), ax...]
    all_gather x1, local copies, waits for them, and re-layouts: 6.52 us -> 2.63 us  [outer_round(): lax.all_gather(outer_new.astype(jnp.bfloat16), 'row')]
where the time goes in v1:
time: 383 us; the launch traced here: 382 us
  waiting for transfers between devices  210 us (55%)
  blocking collectives  54.5 us (14%)
  local copies, waits for them, and re-layouts  41.1 us (11%)
  starting transfers between devices  21.1 us (6%)
  other arithmetic  20.2 us (5%)
  matrix products  19.5 us (5%)
  between operations  15.5 us (4%)
    all_to_all x1, waiting for transfers between devices, outer_round(): lax.all_to_all(pieces, 'col', split_axis=1, concat_axis=1, tiled=True)  97.6 us
    all_to_all x1, waiting for transfers between devices, outer_round(): lax.all_to_all(chosen, 'col', split_axis=1, concat_axis=1, tiled=True)  76.7 us
    all_to_all x1, blocking collectives, sum_at_owner(): lax.all_to_all(blocks, axis, split_axis=0, concat_axis=0, tiled=True)  54.5 us
    all_gather x1, waiting for transfers between devices, outer_round(): lax.all_gather(outer_new.astype(jnp.bfloat16), 'row')  35.8 us
    dot_general x2, matrix products, micro_step(): jnp.dot(normed, params_path[layer], preferred_element_type=jnp.float32)  19.5 us
    all_to_all x1, starting transfers between devices, outer_round(): lax.all_to_all(pieces, 'col', split_axis=1, concat_axis=1, tiled=True)  11.8 us
    reshape x2, local copies, waits for them, and re-layouts, cut_along(): return jnp.moveaxis(shard.reshape(*before, count, -1, *after), dim, 0)  11.8 us
    all_to_all x1, starting transfers between devices, outer_round(): lax.all_to_all(chosen, 'col', split_axis=1, concat_axis=1, tiled=True)  9.24 us
  transfers between devices with their start and end apart: 3, of which 3 were waited for; matrix products, arithmetic and copies ran while one was open for 6% of the time, Pallas kernels for 0%

profile of v1, /device:TPU:1, one launch (start us, length us, event | category | flops | bytes accessed | tf_op | source)
XLA Modules:
  0.0 382.0 jit_solution(12276511717874717873)
XLA Ops:
  7.2 0.7 convert_element_type.60
  7.9 1.3 dynamic_slice.12
  9.1 1.3 dynamic_slice.13
  10.4 0.8 select_reduce_fusion
  11.9 1.2 fusion.49
  13.9 3.3 multiply_convert_fusion
  17.1 2.5 copy.80
  19.6 11.8 %all-to-all-start = ((bf16[2,16,64,1024]{3,2,0,1:T(8,128)(2,1)}), bf16[2,16,64,1024]{3,2,0,1:T(8,128)(2,1)}, u32[]{:S(2)}, u32[]{:S(2)}) async-start(bf16[2,16,64,1024]{3,2,0,1:T(8,128)(2,1)} %copy.80), calls=%async_computation | async-start | bytes 8388608 | tf_op jit(solution)/shard_map/all_to_all | solution.py:23
  31.4 0.0 all-gather.2.cloned.1.call-start
  31.4 0.7 compare_and_fusion
  32.1 0.1 select_reduce_fusion.1
  32.3 97.6 %all-to-all-done = bf16[2,16,64,1024]{3,2,0,1:T(8,128)(2,1)} async-done(((bf16[2,16,64,1024]{3,2,0,1:T(8,128)(2,1)}), bf16[2,16,64,1024]{3,2,0,1:T(8,128)(2,1)}, u32[]{:S(2)}, u32[]{:S(2)}) %all-to-all-start) | async-done | bytes 4194336 | tf_op jit(solution)/shard_map/all_to_all | solution.py:23
  129.9 5.0 %gather_fusion = bf16[16,2,64,1024]{3,2,1,0:T(8,128)(2,1)} fusion(bf16[2,16,64,1024]{3,2,0,1:T(8,128)(2,1)} %all-to-all-done, s32[1024]{0:T(1024)S(1)} %pad_clamp_fusion.1), kind=kCustom, calls=%fused_computation.clone | custom fusion | bytes 8388672 | tf_op jit(solution)/shard_map/jit(_take)/gather | solution.py:24
  134.9 4.7 %select_bitcast_fusion.1 = bf16[2,16,64,1024]{3,2,0,1:T(8,128)(2,1)} fusion(bf16[16,2,64,1024]{3,2,1,0:T(8,128)(2,1)} %gather_fusion, pred[16]{0:T(512)(128)(4,1)S(1)} %compare_and_fusion.1), kind=kLoop, calls=%fused_computation.8 | loop fusion | flops 2097152 | bytes 8388624 | tf_op jit(solution)/shard_map/jit(_take)/select_n | solution.py:24
  139.6 7.2 %reshape.126 = bf16[2,16,16,4,1024]{4,3,2,0,1:T(4,128)(2,1)} reshape(bf16[2,16,64,1024]{3,2,0,1:T(8,128)(2,1)} %select_bitcast_fusion.1) | data formatting | bytes 8388608 | tf_op jit(solution)/shard_map/reshape | solution.py:9
  146.8 4.6 %copy.116 = bf16[2,16,16,4,1024]{4,3,0,1,2:T(4,128)(2,1)S(1)} copy(bf16[2,16,16,4,1024]{4,3,2,0,1:T(4,128)(2,1)} %reshape.126) | data formatting | bytes 8388608 | tf_op jit(solution)/shard_map/reshape | solution.py:9
  151.3 54.5 %all_to_all.15 = bf16[16,2,16,4,1024]{4,3,1,2,0:T(4,128)(2,1)S(1)} all-to-all(bf16[16,2,16,4,1024]{4,3,1,2,0:T(4,128)(2,1)S(1)} %bitcast.79), channel_id=1, replica_groups=mesh['row'=16,'col'=16] {'row'}, dimensions={0} | all-to-all | bytes 8388608 | tf_op jit(solution)/shard_map/all_to_all | solution.py:14
  205.8 0.0 copy-start.1
  205.8 0.0 copy-start.2
  205.8 2.2 convert_reduce_fusion
  208.1 0.0 copy-done.1
  208.1 0.0 copy-done.2
  208.1 0.6 fusion.47
  208.7 0.9 copy.85
  209.6 0.0 all-gather.2.cloned.1.call-update
  209.7 35.8 %all-gather.2.cloned.1.call-done = bf16[16,2,16,4,1024]{4,2,3,1,0:T(8,128)(2,1)} async-done(((bf16[1,2,16,4,1024]{4,2,3,1,0:T(8,128)(2,1)}), bf16[16,2,16,4,1024]{4,2,3,1,0:T(8,128)(2,1)}) %all-gather.2.cloned.1.call-update) | async-done | bytes 4194320 | tf_op jit(solution)/shard_map/all_gather | solution.py:29
  245.5 2.6 copy.86
  248.1 4.3 %copy.87 = bf16[2,16,64,1024]{3,2,1,0:T(8,128)(2,1)} copy(bf16[2,16,64,1024]{3,1,2,0:T(8,128)(2,1)S(1)} %bitcast.80) | data formatting | bytes 8388608 | tf_op jit(solution)/shard_map/reshape | solution.py:29
  252.4 4.9 %gather_fusion.1 = bf16[16,2,64,1024]{3,2,1,0:T(8,128)(2,1)} fusion(bf16[2,16,64,1024]{3,2,1,0:T(8,128)(2,1)} %copy.87, s32[1024]{0:T(1024)S(1)} %pad_clamp_fusion), kind=kCustom, calls=%fused_computation.1.clone | custom fusion | bytes 8388672 | tf_op jit(solution)/shard_map/jit(_take)/gather | solution.py:30
  257.4 4.7 %select_bitcast_fusion = bf16[2,16,64,1024]{3,2,0,1:T(8,128)(2,1)} fusion(bf16[16,2,64,1024]{3,2,1,0:T(8,128)(2,1)} %gather_fusion.1, pred[16]{0:T(512)(128)(4,1)S(1)} %get-tuple-element.33), kind=kLoop, calls=%fused_computation.7 | loop fusion | flops 2097152 | bytes 8388624 | tf_op jit(solution)/shard_map/jit(_take)/select_n | solution.py:30
  262.0 0.0 copy-start.3
  262.0 9.2 %all-to-all-start.2 = ((bf16[2,16,64,1024]{3,2,0,1:T(8,128)(2,1)}), bf16[2,16,64,1024]{3,2,0,1:T(8,128)(2,1)}, u32[]{:S(2)}, u32[]{:S(2)}) async-start(bf16[2,16,64,1024]{3,2,0,1:T(8,128)(2,1)} %select_bitcast_fusion), calls=%async_computation.2 | async-start | bytes 8388608 | tf_op jit(solution)/shard_map/all_to_all | solution.py:31
  271.3 0.0 copy-done.3
  271.3 0.4 fusion.2
  271.7 0.0 copy-start
  271.7 10.1 %multiply_reduce_fusion = (f32[736]{0:T(1024)S(1)}, f32[736,1024]{1,0:T(8,128)S(1)}) fusion(bf16[1,1,2,1024,1024]{4,3,2,1,0:T(8,128)(2,1)} %param.9, bf16[1,1,736,1024]{3,2,1,0:T(8,128)(2,1)S(1)} %copy-done.3, f32[736]{0:T(1024)S(1)} %add_rsqrt_fusion.1), kind=kOutput, calls=%fused_computation.35 | convolution fusion | flops 1597013248 | bytes 8133504 | tf_op jit(solution)/shard_map/dot_general | solution.py:40
  281.7 0.0 copy-done
  281.7 9.4 %fusion.36 = bf16[1,1,736,1024]{3,2,1,0:T(8,128)(2,1)} fusion(f32[736,1024]{1,0:T(8,128)S(1)} %get-tuple-element.38, bf16[1,1,2,1024,1024]{4,3,2,1,0:T(8,128)(2,1)S(1)} %copy-done, f32[736]{0:T(1024)S(1)} %add_rsqrt_fusion), kind=kOutput, calls=%fused_computation.62 | convolution fusion | flops 1594753024 | bytes 9637888 | tf_op jit(solution)/shard_map/dot_general | solution.py:40
  291.2 0.7 fusion.48
  291.8 0.8 copy.91
  292.7 0.8 copy.92
  293.5 76.7 %all-to-all-done.2 = bf16[2,16,64,1024]{3,2,0,1:T(8,128)(2,1)} async-done(((bf16[2,16,64,1024]{3,2,0,1:T(8,128)(2,1)}), bf16[2,16,64,1024]{3,2,0,1:T(8,128)(2,1)}, u32[]{:S(2)}, u32[]{:S(2)}) %all-to-all-start.2) | async-done | bytes 4194336 | tf_op jit(solution)/shard_map/all_to_all | solution.py:31
  370.3 4.9 %copy.88 = bf16[2,16,64,1024]{3,2,1,0:T(8,128)(2,1)} copy(bf16[2,16,64,1024]{3,2,0,1:T(8,128)(2,1)} %all-to-all-done.2) | data formatting | bytes 8388608 | tf_op jit(solution)/shard_map/all_to_all | solution.py:31
  (7 shorter events, 0.0 us)
Async XLA Ops:
  19.6 110.3 %all-to-all-start = ((bf16[2,16,64,1024]{3,2,0,1:T(8,128)(2,1)}), bf16[2,16,64,1024]{3,2,0,1:T(8,128)(2,1)}, u32[]{:S(2)}, u32[]{:S(2)}) async-start(bf16[2,16,64,1024]{3,2,0,1:T(8,128)(2,1)} %copy.80), calls=%async_computation | async-start | bytes 8388608 | tf_op jit(solution)/shard_map/all_to_all | solution.py:23
  31.4 214.1 %all-gather.2.cloned.1.call-start = ((), (), s32[]{:S(2)}) async-start(), calls=%async_computation.3 | async-start | bytes 4456448 | tf_op jit(solution)/shard_map/all_gather | solution.py:29
  205.8 2.3 copy-start.1
  205.8 2.3 copy-start.2
  262.0 9.3 %copy-start.3 = (bf16[1,1,736,1024]{3,2,1,0:T(8,128)(2,1)S(1)}, bf16[1,1,736,1024]{3,2,1,0:T(8,128)(2,1)}, u32[]{:S(2)}) copy-start(bf16[1,1,736,1024]{3,2,1,0:T(8,128)(2,1)} %param.8) | copy-start | bytes 4521988
  262.0 108.2 %all-to-all-start.2 = ((bf16[2,16,64,1024]{3,2,0,1:T(8,128)(2,1)}), bf16[2,16,64,1024]{3,2,0,1:T(8,128)(2,1)}, u32[]{:S(2)}, u32[]{:S(2)}) async-start(bf16[2,16,64,1024]{3,2,0,1:T(8,128)(2,1)} %select_bitcast_fusion), calls=%async_computation.2 | async-start | bytes 8388608 | tf_op jit(solution)/shard_map/all_to_all | solution.py:31
  271.7 10.1 %copy-start = (bf16[1,1,2,1024,1024]{4,3,2,1,0:T(8,128)(2,1)S(1)}, bf16[1,1,2,1024,1024]{4,3,2,1,0:T(8,128)(2,1)}, u32[]{:S(2)}) copy-start(bf16[1,1,2,1024,1024]{4,3,2,1,0:T(8,128)(2,1)} %param.9) | copy-start | bytes 12582916
Sparse Core Ops, SparseCore 0:
  209.7 35.6 all-gather.1
